TPU v7x, 32 devices: a whole 2x2x4 slice. The times are simulated.
32 devices in a mesh: blk: 4 (over x, core), grp: 8 (over z, y).
Axes of the slice: x: 2, y: 2, z: 4, core: 2. Of those that a mesh axis runs over, the one named last changes fastest.
Arguments:
- design: float32 [8, 4096], P(None, ('blk', 'grp')), may hold values from -5 to 5
- lengthscales: float32 [8], replicated, may hold values from 0.55 to 0.85
- counts: int32 [4096], P(('blk', 'grp')), may hold values from 1 to 16
- noise_base: float32 [1], replicated, may hold values from 0.5 to 2
- targets: float32 [16, 4096], P(None, ('blk', 'grp')), may hold values from -6 to 6
Outputs:
- solution: float32 [16, 4096], P(None, ('blk', 'grp'))
- residual: float32 [16, 4096], P(None, ('blk', 'grp'))
- image: float32 [16, 4096], P(None, ('blk', 'grp'))
All inputs are finite; a program needn't handle non-finite values.
Results may differ from a plain program's by a relative error of at most 0.0003.
Values sent between devices are 32-bit elements; how exact they have to be, the bound alone decides.
No kernel may reach another device: no remote copies, remote signals or barrier semaphores. Data moves between devices by JAX's collectives and lax.ppermute only.
A program may use at most 64 MiB of HBM per device.

v0:
```python
import math
import jax
import jax.numpy as jnp
from jax import lax
from jax.sharding import PartitionSpec as P

ROOT_FIVE = 2.23606797749979


def kernel_terms(own_scaled, own_square, col_scaled, col_dirs, running):
    columns = col_scaled.shape[1]
    block_width = math.gcd(columns, 2048)
    block_count = columns // block_width

    def advance(block_index, partial_sum):
        offset = block_index * block_width
        chosen = lax.dynamic_slice_in_dim(col_scaled, offset, block_width, 1)
        chosen_dirs = lax.dynamic_slice_in_dim(col_dirs, offset, block_width, 1)
        chosen_square = jnp.sum(chosen * chosen, 0)
        inner_products = jnp.einsum(
            "dr,dc->rc", own_scaled, chosen, precision=lax.Precision.HIGHEST
        )
        dist_square = jnp.maximum(
            own_square[:, None] + chosen_square[None, :] - 2.0 * inner_products, 0.0
        )
        radius = jnp.sqrt(dist_square)
        kernel_tile = (1.0 + ROOT_FIVE * radius + 5.0 / 3.0 * dist_square) * jnp.exp(
            -ROOT_FIVE * radius
        )
        return partial_sum + jnp.einsum(
            "kc,rc->kr", chosen_dirs, kernel_tile, precision=lax.Precision.HIGHEST
        )

    return lax.fori_loop(0, block_count, advance, running)


def on_device(design, lengthscales, counts, noise_base, targets):
    scaled = design / lengthscales[:, None]
    own_square = jnp.sum(scaled * scaled, 0)
    noise_diag = noise_base[0] / counts.astype(jnp.float32)

    def operator_apply(direction):
        zero_start = jnp.zeros(direction.shape, jnp.float32)
        group_points, group_dirs = (
            lax.all_gather(scaled, "grp", axis=1, tiled=True),
            lax.all_gather(direction, "grp", axis=1, tiled=True),
        )
        product_sum = kernel_terms(
            scaled,
            own_square,
            lax.all_gather(group_points, "blk", axis=1, tiled=True),
            lax.all_gather(group_dirs, "blk", axis=1, tiled=True),
            zero_start,
        )
        return product_sum + noise_diag[None, :] * direction

    first = operator_apply(targets)
    local_gammas = jnp.sum(targets * targets, 1)
    local_deltas = jnp.sum(first * targets, 1)
    gammas, deltas = lax.psum((local_gammas, local_deltas), ("blk", "grp"))
    further = operator_apply(first)
    alphas = (gammas / deltas)[:, None]
    solution = alphas * targets
    residual = targets - alphas * first
    image = first - alphas * further
    return (solution, residual, image)


def solution(mesh):
    in_specs = (P(None, ("blk", "grp")), P(), P(("blk", "grp")), P(), P(None, ("blk", "grp")))
    out_specs = (P(None, ("blk", "grp")), P(None, ("blk", "grp")), P(None, ("blk", "grp")))
    return jax.shard_map(
        on_device, mesh=mesh, in_specs=in_specs, out_specs=out_specs, check_vma=False
    )
```

profile of v0, /device:TPU:0, one launch (start us, length us, event | category | flops | bytes accessed | tf_op | source)
XLA Modules:
  0.0 167.1 jit_solution(15107459266311778984)
XLA Ops:
  0.6 0.0 copy-start.1
  1.3 0.0 copy-start.3
  1.3 0.6 copy-done.3
  2.0 0.6 copy-done.2
  2.6 0.1 multiply_reduce_fusion.4
  2.7 32.6 %all_gather.22 = f32[8,1024]{1,0:T(8,128)S(1)} all-gather(f32[8,128]{1,0:T(8,128)S(1)} %get-tuple-element.408), channel_id=1, replica_groups=mesh['blk'=4,'grp'=8] {'grp'}, dimensions={1}, use_global_device_ids=true | all-gather | bytes 36864 | tf_op jit(solution)/shard_map/all_gather | solution.py:45
  35.3 30.5 %all_gather.20 = f32[16,1024]{1,0:T(8,128)S(1)} all-gather(f32[16,128]{1,0:T(8,128)S(1)} %copy-done), channel_id=1, replica_groups=mesh['blk'=4,'grp'=8] {'grp'}, dimensions={1}, use_global_device_ids=true | all-gather | bytes 73728 | tf_op jit(solution)/shard_map/all_gather | solution.py:46
  65.8 5.4 %all_gather.23 = f32[8,4096]{1,0:T(8,128)S(1)} all-gather(f32[8,1024]{1,0:T(8,128)S(1)} %all_gather.22), channel_id=1, replica_groups=mesh['blk'=4,'grp'=8] {'blk'}, dimensions={1}, use_global_device_ids=true | all-gather | bytes 163840 | tf_op jit(solution)/shard_map/all_gather | solution.py:51
  71.2 5.8 %all_gather.21 = f32[16,4096]{1,0:T(8,128)S(1)} all-gather(f32[16,1024]{1,0:T(8,128)S(1)} %all_gather.20), channel_id=1, replica_groups=mesh['blk'=4,'grp'=8] {'blk'}, dimensions={1}, use_global_device_ids=true | all-gather | bytes 327680 | tf_op jit(solution)/shard_map/all_gather | solution.py:52
  77.0 6.3 %while.28 = (s32[]{:T(128)}, f32[16,128]{1,0:T(8,128)S(1)}, f32[16,4096]{1,0:T(8,128)S(1)}, f32[128]{0:T(128)S(1)}, f32[8,4096]{1,0:T(8,128)S(1)}, /*index=5*/f3...) while((s32[]{:T(128)}, f32[16,128]{1,0:T(8,128)S(1)}, ...), condition=%wide.region_5.0_spmd.clone, body=%wide.region_3.5_spmd.clone.sunk | while | flops 78153728 | bytes 2396849 | solution.py:34
  77.1 2.0 %fusion.62 = f32[128,2048]{0,1:T(8,128)S(1)} fusion(f32[8,128]{1,0:T(8,128)S(1)} %get-tuple-element.398, f32[2048]{0:T(1024)S(1)} %multiply_reduce_fusion.7, f32[128]{0:T(128)S(1)} %get-tuple-element.396, f32[8,4096]{1,0:T(8,128)S(1)} %get-tuple-element.397, s32[]{:T(128)S(6)} %select_n.20), kind=kOutput, calls=%fused_computation.3.clone.1 | convolution fusion | flops 26214400 | bytes 1126916 | tf_op jit(solution)/shard_map/while/body/eval_jaxpr/dr,dc->rc/dot_general | solution.py:20
  79.1 1.1 convolution_add_fusion.4
  80.2 2.0 %fusion.62 = f32[128,2048]{0,1:T(8,128)S(1)} fusion(f32[8,128]{1,0:T(8,128)S(1)} %get-tuple-element.398, f32[2048]{0:T(1024)S(1)} %multiply_reduce_fusion.7, f32[128]{0:T(128)S(1)} %get-tuple-element.396, f32[8,4096]{1,0:T(8,128)S(1)} %get-tuple-element.397, s32[]{:T(128)S(6)} %select_n.20), kind=kOutput, calls=%fused_computation.3.clone.1 | convolution fusion | flops 26214400 | bytes 1126916 | tf_op jit(solution)/shard_map/while/body/eval_jaxpr/dr,dc->rc/dot_general | solution.py:20
  82.2 1.1 convolution_add_fusion.4
  83.4 0.1 multiply_reduce_fusion.2
  83.5 39.5 %all-reduce = (f32[16]{0:T(128)S(1)}, f32[16]{0:T(128)S(1)}) all-reduce(f32[16]{0:T(128)S(1)} %get-tuple-element.266, f32[16]{0:T(128)S(1)} %get-tuple-element.265), channel_id=1, replica_groups=mesh['blk'=4,'grp'=8] {'blk','grp'}, use_global_device_ids=true, to_apply=%region_1.2 | all-reduce | flops 32 | bytes 256 | tf_op jit(solution)/shard_map/psum | solution.py:60
  123.0 30.5 %all_gather.24 = f32[16,1024]{1,0:T(8,128)S(1)} all-gather(f32[16,128]{1,0:T(8,128)S(1)} %get-tuple-element.293), channel_id=1, replica_groups=mesh['blk'=4,'grp'=8] {'grp'}, dimensions={1}, use_global_device_ids=true | all-gather | bytes 73728 | tf_op jit(solution)/shard_map/all_gather | solution.py:46
  153.6 6.5 %all_gather.25 = f32[16,4096]{1,0:T(8,128)S(1)} all-gather(f32[16,1024]{1,0:T(8,128)S(1)} %all_gather.24), channel_id=1, replica_groups=mesh['blk'=4,'grp'=8] {'blk'}, dimensions={1}, use_global_device_ids=true | all-gather | bytes 327680 | tf_op jit(solution)/shard_map/all_gather | solution.py:52
  160.1 6.3 %while.29 = (s32[]{:T(128)}, f32[16,128]{1,0:T(8,128)S(1)}, f32[16,4096]{1,0:T(8,128)S(1)}, f32[128]{0:T(128)S(1)}, f32[8,4096]{1,0:T(8,128)S(1)}, /*index=5*/f3...) while((s32[]{:T(128)}, f32[16,128]{1,0:T(8,128)S(1)}, ...), condition=%wide.region_10.0_spmd.clone, body=%wide.region_8.0_spmd.clone.sunk | while | flops 78153728 | bytes 2396849 | solution.py:34
  160.1 2.0 %fusion.67 = f32[128,2048]{0,1:T(8,128)S(1)} fusion(f32[8,128]{1,0:T(8,128)S(1)} %get-tuple-element.428, f32[2048]{0:T(1024)S(1)} %multiply_reduce_fusion.8, f32[128]{0:T(128)S(1)} %get-tuple-element.426, f32[8,4096]{1,0:T(8,128)S(1)} %get-tuple-element.427, s32[]{:T(128)S(6)} %select_n.21), kind=kOutput, calls=%fused_computation.29.clone.1 | convolution fusion | flops 26214400 | bytes 1126916 | tf_op jit(solution)/shard_map/while/body/eval_jaxpr/dr,dc->rc/dot_general | solution.py:20
  162.1 1.1 convolution_add_fusion.5
  163.3 2.0 %fusion.67 = f32[128,2048]{0,1:T(8,128)S(1)} fusion(f32[8,128]{1,0:T(8,128)S(1)} %get-tuple-element.428, f32[2048]{0:T(1024)S(1)} %multiply_reduce_fusion.8, f32[128]{0:T(128)S(1)} %get-tuple-element.426, f32[8,4096]{1,0:T(8,128)S(1)} %get-tuple-element.427, s32[]{:T(128)S(6)} %select_n.21), kind=kOutput, calls=%fused_computation.29.clone.1 | convolution fusion | flops 26214400 | bytes 1126916 | tf_op jit(solution)/shard_map/while/body/eval_jaxpr/dr,dc->rc/dot_general | solution.py:20
  165.3 1.1 convolution_add_fusion.5
  166.4 0.7 multiply_subtract_fusion
  (12 shorter events, 0.1 us)
Async XLA Ops:
  0.6 1.3 copy-start.1
  1.3 0.7 copy-start.3
  2.0 0.7 copy-start.2
  2.7 32.6 %copy-start = (f32[16,128]{1,0:T(8,128)S(1)}, f32[16,128]{1,0:T(8,128)}, u32[]{:S(2)}) copy-start(f32[16,128]{1,0:T(8,128)} %param.13) | copy-start | bytes 24580
where the time goes:
time: 168 us; the launch traced here: 167 us
  blocking collectives  151 us (90%)
  matrix products  12.4 us (7%)
    all_gather x2, blocking collectives, operator_apply(): lax.all_gather(direction, 'grp', axis=1, tiled=True)  61.1 us
    psum x1, blocking collectives, on_device(): gammas, deltas = lax.psum((local_gammas, local_deltas), ('blk', 'grp'))  39.5 us
    all_gather x1, blocking collectives, operator_apply(): lax.all_gather(scaled, 'grp', axis=1, tiled=True)  32.6 us
    all_gather x2, blocking collectives, operator_apply(): lax.all_gather(group_dirs, 'blk', axis=1, tiled=True)  12.4 us
    dot_general x4, matrix products, advance(): jnp.einsum('dr,dc->rc', own_scaled, chosen, precision=lax.Precision.HIGHEST)  7.95 us
    all_gather x1, blocking collectives, operator_apply(): lax.all_gather(group_points, 'blk', axis=1, tiled=True)  5.4 us
    dot_general x4, matrix products, advance(): jnp.einsum('kc,rc->kr', chosen_dirs, kernel_tile, precision=lax.Precision...  4.49 us

commit v1 on v0

--- a/solution.py
+++ b/solution.py
@@ -5,6 +5,9 @@
 from jax.sharding import PartitionSpec as P
 
 ROOT_FIVE = 2.23606797749979
+note_panels_in = lambda row_dim, u_in, axis_name: jnp.concatenate(
+    lax.all_gather(u_in, axis_name=axis_name), axis=row_dim
+)
 
 
 def kernel_terms(own_scaled, own_square, col_scaled, col_dirs, running):
@@ -49,7 +52,7 @@
             scaled,
             own_square,
             lax.all_gather(group_points, "blk", axis=1, tiled=True),
-            lax.all_gather(group_dirs, "blk", axis=1, tiled=True),
+            note_panels_in(1, u_in=group_dirs, axis_name="blk"),
             zero_start,
         )
         return product_sum + noise_diag[None, :] * direction

time: 168 us -> 168 us (level)
  no operation moved by 1% of the time
where the time goes in v1:
time: 168 us
  blocking collectives  151 us (90%)
  matrix products  12.4 us (7%)
    all_gather x2, blocking collectives, operator_apply(): lax.all_gather(direction, 'grp', axis=1, tiled=True)  61.1 us
    psum x1, blocking collectives, on_device(): gammas, deltas = lax.psum((local_gammas, local_deltas), ('blk', 'grp'))  39.5 us
    all_gather x1, blocking collectives, operator_apply(): lax.all_gather(scaled, 'grp', axis=1, tiled=True)  32.6 us
    all_gather x2, blocking collectives, lax.all_gather(u_in, axis_name=axis_name)  12.4 us
    dot_general x4, matrix products, advance(): jnp.einsum('dr,dc->rc', own_scaled, chosen, precision=lax.Precision.HIGHEST)  7.95 us
    all_gather x1, blocking collectives, operator_apply(): lax.all_gather(group_points, 'blk', axis=1, tiled=True)  5.4 us
    dot_general x4, matrix products, advance(): jnp.einsum('kc,rc->kr', chosen_dirs, kernel_tile, precision=lax.Precision...  4.49 us

profile of v1, /device:TPU:0, one launch (start us, length us, event | category | flops | bytes accessed | tf_op | source)
XLA Modules:
  0.0 167.5 jit_solution(9326192220234191441)
XLA Ops:
  1.3 0.6 copy-done.3
  2.0 0.6 copy-done.2
  2.6 0.1 multiply_reduce_fusion.4
  2.7 32.6 %all_gather.29 = f32[8,1024]{1,0:T(8,128)S(1)} all-gather(f32[8,128]{1,0:T(8,128)S(1)} %get-tuple-element.408), channel_id=1, replica_groups=mesh['blk'=4,'grp'=8] {'grp'}, dimensions={1}, use_global_device_ids=true | all-gather | bytes 36864 | tf_op jit(solution)/shard_map/all_gather | solution.py:48
  35.3 30.5 %all_gather.26 = f32[16,1024]{1,0:T(8,128)S(1)} all-gather(f32[16,128]{1,0:T(8,128)S(1)} %copy-done), channel_id=1, replica_groups=mesh['blk'=4,'grp'=8] {'grp'}, dimensions={1}, use_global_device_ids=true | all-gather | bytes 73728 | tf_op jit(solution)/shard_map/all_gather | solution.py:49
  65.8 5.4 %all_gather.30 = f32[8,4096]{1,0:T(8,128)S(1)} all-gather(f32[8,1024]{1,0:T(8,128)S(1)} %all_gather.29), channel_id=1, replica_groups=mesh['blk'=4,'grp'=8] {'blk'}, dimensions={1}, use_global_device_ids=true | all-gather | bytes 163840 | tf_op jit(solution)/shard_map/all_gather | solution.py:54
  71.2 5.8 %all-gather = f32[64,1024]{1,0:T(8,128)S(1)} all-gather(f32[16,1024]{1,0:T(8,128)S(1)} %all_gather.26), channel_id=2, replica_groups=mesh['blk'=4,'grp'=8] {'blk'}, dimensions={0}, use_global_device_ids=true | all-gather | bytes 327680 | tf_op jit(solution)/shard_map/all_gather | solution.py:9
  77.0 0.2 copy.8
  77.2 0.2 copy.11
  77.4 6.4 %while.28 = (s32[]{:T(128)}, f32[16,128]{1,0:T(8,128)S(1)}, f32[16,4096]{1,0:T(8,128)S(1)}, f32[128]{0:T(128)S(1)}, f32[8,4096]{1,0:T(8,128)S(1)}, /*index=5*/f3...) while((s32[]{:T(128)}, f32[16,128]{1,0:T(8,128)S(1)}, ...), condition=%wide.region_5.0_spmd.clone, body=%wide.region_3.5_spmd.clone.sunk | while | flops 78153728 | bytes 2396849 | solution.py:37
  77.4 2.0 %fusion.62 = f32[128,2048]{0,1:T(8,128)S(1)} fusion(f32[8,128]{1,0:T(8,128)S(1)} %get-tuple-element.398, f32[2048]{0:T(1024)S(1)} %multiply_reduce_fusion.7, f32[128]{0:T(128)S(1)} %get-tuple-element.396, f32[8,4096]{1,0:T(8,128)S(1)} %get-tuple-element.397, s32[]{:T(128)S(6)} %select_n.20), kind=kOutput, calls=%fused_computation.3.clone.1 | convolution fusion | flops 26214400 | bytes 1126916 | tf_op jit(solution)/shard_map/while/body/eval_jaxpr/dr,dc->rc/dot_general | solution.py:23
  79.4 1.1 convolution_add_fusion.4
  80.6 2.0 %fusion.62 = f32[128,2048]{0,1:T(8,128)S(1)} fusion(f32[8,128]{1,0:T(8,128)S(1)} %get-tuple-element.398, f32[2048]{0:T(1024)S(1)} %multiply_reduce_fusion.7, f32[128]{0:T(128)S(1)} %get-tuple-element.396, f32[8,4096]{1,0:T(8,128)S(1)} %get-tuple-element.397, s32[]{:T(128)S(6)} %select_n.20), kind=kOutput, calls=%fused_computation.3.clone.1 | convolution fusion | flops 26214400 | bytes 1126916 | tf_op jit(solution)/shard_map/while/body/eval_jaxpr/dr,dc->rc/dot_general | solution.py:23
  82.6 1.1 convolution_add_fusion.4
  83.7 0.1 multiply_reduce_fusion.2
  83.9 39.5 %all-reduce = (f32[16]{0:T(128)S(1)}, f32[16]{0:T(128)S(1)}) all-reduce(f32[16]{0:T(128)S(1)} %get-tuple-element.266, f32[16]{0:T(128)S(1)} %get-tuple-element.265), channel_id=1, replica_groups=mesh['blk'=4,'grp'=8] {'blk','grp'}, use_global_device_ids=true, to_apply=%region_1.2 | all-reduce | flops 32 | bytes 256 | tf_op jit(solution)/shard_map/psum | solution.py:63
  123.4 30.5 %all_gather.31 = f32[16,1024]{1,0:T(8,128)S(1)} all-gather(f32[16,128]{1,0:T(8,128)S(1)} %get-tuple-element.293), channel_id=1, replica_groups=mesh['blk'=4,'grp'=8] {'grp'}, dimensions={1}, use_global_device_ids=true | all-gather | bytes 73728 | tf_op jit(solution)/shard_map/all_gather | solution.py:49
  153.9 6.5 %all-gather.1 = f32[64,1024]{1,0:T(8,128)S(1)} all-gather(f32[16,1024]{1,0:T(8,128)S(1)} %all_gather.31), channel_id=3, replica_groups=mesh['blk'=4,'grp'=8] {'blk'}, dimensions={0}, use_global_device_ids=true | all-gather | bytes 327680 | tf_op jit(solution)/shard_map/all_gather | solution.py:9
  160.5 6.4 %while.29 = (s32[]{:T(128)}, f32[16,128]{1,0:T(8,128)S(1)}, f32[16,4096]{1,0:T(8,128)S(1)}, f32[128]{0:T(128)S(1)}, f32[8,4096]{1,0:T(8,128)S(1)}, /*index=5*/f3...) while((s32[]{:T(128)}, f32[16,128]{1,0:T(8,128)S(1)}, ...), condition=%wide.region_10.0_spmd.clone, body=%wide.region_8.0_spmd.clone.sunk | while | flops 78153728 | bytes 2396849 | solution.py:37
  160.5 2.0 %fusion.67 = f32[128,2048]{0,1:T(8,128)S(1)} fusion(f32[8,128]{1,0:T(8,128)S(1)} %get-tuple-element.428, f32[2048]{0:T(1024)S(1)} %multiply_reduce_fusion.8, f32[128]{0:T(128)S(1)} %get-tuple-element.426, f32[8,4096]{1,0:T(8,128)S(1)} %get-tuple-element.427, s32[]{:T(128)S(6)} %select_n.21), kind=kOutput, calls=%fused_computation.29.clone.1 | convolution fusion | flops 26214400 | bytes 1126916 | tf_op jit(solution)/shard_map/while/body/eval_jaxpr/dr,dc->rc/dot_general | solution.py:23
  162.5 1.1 convolution_add_fusion.5
  163.7 2.0 %fusion.67 = f32[128,2048]{0,1:T(8,128)S(1)} fusion(f32[8,128]{1,0:T(8,128)S(1)} %get-tuple-element.428, f32[2048]{0:T(1024)S(1)} %multiply_reduce_fusion.8, f32[128]{0:T(128)S(1)} %get-tuple-element.426, f32[8,4096]{1,0:T(8,128)S(1)} %get-tuple-element.427, s32[]{:T(128)S(6)} %select_n.21), kind=kOutput, calls=%fused_computation.29.clone.1 | convolution fusion | flops 26214400 | bytes 1126916 | tf_op jit(solution)/shard_map/while/body/eval_jaxpr/dr,dc->rc/dot_general | solution.py:23
  165.7 1.1 convolution_add_fusion.5
  166.9 0.7 multiply_subtract_fusion
  (15 shorter events, 0.2 us)
Async XLA Ops:
  0.6 1.3 copy-start.1
  1.3 0.7 copy-start.3
  2.0 0.7 copy-start.2
  2.7 32.6 %copy-start = (f32[16,128]{1,0:T(8,128)S(1)}, f32[16,128]{1,0:T(8,128)}, u32[]{:S(2)}) copy-start(f32[16,128]{1,0:T(8,128)} %param.13) | copy-start | bytes 24580
